TPU v7x, 32 devices: a whole 2x2x4 slice. The times are simulated.
32 devices in a mesh: rows: 8 (over y, x, core), feat: 4 (over z).
Axes of the slice: x: 2, y: 2, z: 4, core: 2. Of those that a mesh axis runs over, the one named last changes fastest.
Arguments:
- features: bfloat16 [8192, 2048], P('rows', 'feat'), may hold values from -6 to 6
- grad_out: bfloat16 [8192, 2048], P('rows', 'feat'), may hold values from -6 to 6
- eigvecs: float32 [2048, 2048], P('feat', 'rows'), may hold values from -1 to 1, as said below
- eigvals: float32 [2048], replicated, may hold values from 0.1 to 1, as said below
- whiten: bfloat16 [2048, 2048], P(None, 'feat'), may hold values from -0.125 to 0.125
Outputs:
- grad_in: bfloat16 [8192, 2048], P('rows', 'feat')
Inputs may be any that keep to these rules, and one draw needn't show every extreme that they name: `eigvecs`: the columns are orthonormal. `eigvals`: any two entries differ by at least 0.45 / 2048.
All inputs are finite; a program needn't handle non-finite values.
Results may differ from a plain program's by a relative error of at most 0.0074.
Values may be sent and summed in bfloat16 or wider, within the bound.
A program may use at most 128 MiB of HBM per device.

v0:
```python
import jax
import jax.numpy as jnp
from jax import lax
from jax.sharding import PartitionSpec as P


def divided(lam_row, lam_col, first_col):
    on_diag = (
        jnp.arange(lam_row.shape[0], dtype=jnp.int32)[:, None]
        == (first_col + jnp.arange(lam_col.shape[0], dtype=jnp.int32))[None, :]
    )
    root_row = lam_row ** (-0.5)
    root_col = lam_col ** (-0.5)
    gaps_lam = lam_row[:, None] - lam_col[None, :]
    safe_gap = jnp.where(on_diag, jnp.ones_like(gaps_lam), gaps_lam)
    off_diag = (root_row[:, None] - root_col[None, :]) / safe_gap
    diag_vals = -0.5 * lam_row[:, None] ** (-1.5) + jnp.zeros_like(gaps_lam)
    return jnp.where(on_diag, diag_vals, off_diag)


def local(features, grad_out, eigvecs, eigvals, whiten):
    highest = lax.Precision.HIGHEST
    tok_rows, own_cols = features.shape
    row_count = tok_rows * lax.axis_size("rows")
    contract_rows = (((0,), (0,)), ((), ()))
    contract_last = (((1,), (1,)), ((), ()))
    piece_x = lax.all_gather(features, "feat", axis=1, tiled=True)
    piece_g = lax.all_gather(grad_out, "feat", axis=1, tiled=True)
    left_part = lax.dot_general(
        features, piece_g, contract_rows, preferred_element_type=jnp.float32
    )
    right_part = lax.dot_general(
        grad_out, piece_x, contract_rows, preferred_element_type=jnp.float32
    )
    cross_one = left_part
    cross_two = right_part
    sum_x = jnp.sum(piece_x, axis=0, dtype=jnp.float32)
    sum_g = jnp.sum(piece_g, axis=0, dtype=jnp.float32)
    cross_one, cross_two, sum_x, sum_g = (cross_one, cross_two, sum_x, sum_g)
    cross_one, cross_two, sum_x, sum_g = lax.psum((cross_one, cross_two, sum_x, sum_g), "rows")
    both_cross = cross_one + cross_two
    col_mean = sum_x / row_count
    grad_mean = sum_g / row_count
    offset = lax.axis_index("feat") * own_cols
    mean_part = lax.dynamic_slice_in_dim(col_mean, offset, own_cols)
    grad_part = lax.dynamic_slice_in_dim(grad_mean, offset, own_cols)
    sym_gram = 0.5 * (
        both_cross
        - row_count
        * (mean_part[:, None] * grad_mean[None, :] + grad_part[:, None] * col_mean[None, :])
    )
    basis_cols = lax.all_gather(eigvecs, "feat", axis=0, tiled=True)
    basis_block = lax.all_gather(eigvecs, "rows", axis=1, tiled=True)
    narrow = basis_cols.shape[1]
    inner_prod = jnp.dot(sym_gram, basis_cols, precision=highest)
    partial_value = lax.dot_general(basis_block, inner_prod, contract_rows, precision=highest)
    rotated = lax.psum(partial_value, "feat")
    first_col = lax.axis_index("rows") * narrow
    lam_col = lax.dynamic_slice_in_dim(eigvals, first_col, narrow)
    scaled = divided(eigvals, lam_col, first_col) * rotated
    back_rot = jnp.dot(basis_block, scaled, precision=highest)
    sens_own = lax.psum_scatter(
        lax.dot_general(back_rot, basis_cols, contract_last, precision=highest),
        "rows",
        scatter_dimension=0,
        tiled=True,
    )
    scaled_own = (2.0 / row_count * sens_own).astype(jnp.bfloat16)
    sens_scaled = lax.all_gather(scaled_own, "rows", axis=0, tiled=True)
    piece_x = lax.all_gather(features, "feat", axis=1, tiled=True)
    piece_g = lax.all_gather(grad_out, "feat", axis=1, tiled=True)
    shifted = (piece_g.astype(jnp.float32) - grad_mean).astype(jnp.bfloat16)
    centered = (piece_x.astype(jnp.float32) - col_mean).astype(jnp.bfloat16)
    running = jnp.dot(shifted, whiten, preferred_element_type=jnp.float32)
    grad_in = running + lax.dot_general(
        centered, sens_scaled, contract_last, preferred_element_type=jnp.float32
    )
    return grad_in.astype(jnp.bfloat16)


def solution(mesh):
    in_specs = (P("rows", "feat"), P("rows", "feat"), P("feat", "rows"), P(), P(None, "feat"))
    out_specs = P("rows", "feat")
    return jax.shard_map(local, mesh=mesh, in_specs=in_specs, out_specs=out_specs, check_vma=False)
```

profile of v0, /device:TPU:0, one launch (start us, length us, event | category | flops | bytes accessed | tf_op | source)
XLA Modules:
  0.0 552.3 jit_solution(13871746332786428748)
XLA Ops:
  6.5 0.0 copy-start
  6.5 0.0 all-gather.6.cloned.1.call-start
  6.5 0.7 all-gather.6.cloned.1.call-update
  7.3 0.0 all-gather.8.cloned.1.call-start
  7.3 0.7 all-gather.8.cloned.1.call-update
  8.0 0.0 all-gather.10.cloned.1.call-start
  8.1 0.7 all-gather.10.cloned.1.call-update
  8.7 0.0 copy-start.3
  8.8 0.0 all-reduce.6.cloned.1.call-start
  8.8 83.6 %all-gather.6.cloned.1.call-done = bf16[1024,2048]{1,0:T(8,128)(2,1)} async-done(((bf16[1024,512]{1,0:T(8,128)(2,1)}), bf16[1024,2048]{1,0:T(8,128)(2,1)}) %all-gather.6.cloned.1.call-update) | async-done | bytes 4194320 | tf_op jit(solution)/shard_map/all_gather | solution.py:71
  92.4 6.8 %fusion.40 = f32[512,2048]{1,0:T(8,128)} fusion(bf16[1024,512]{1,0:T(8,128)(2,1)} %param.5, bf16[1024,2048]{1,0:T(8,128)(2,1)} %all-gather.6.cloned.1.call-done), kind=kOutput, calls=%fused_computation.51 | convolution fusion | flops 2147483648 | bytes 9437184 | tf_op jit(solution)/shard_map/dot_general | solution.py:29
  99.2 74.0 %all-gather.8.cloned.1.call-done = bf16[1024,2048]{1,0:T(8,128)(2,1)} async-done(((bf16[1024,512]{1,0:T(8,128)(2,1)}), bf16[1024,2048]{1,0:T(8,128)(2,1)}) %all-gather.8.cloned.1.call-update) | async-done | bytes 4194320 | tf_op jit(solution)/shard_map/all_gather | solution.py:70
  173.2 0.0 copy-done.3
  173.2 7.8 %convolution_add_fusion = f32[512,2048]{1,0:T(8,128)} fusion(f32[512,2048]{1,0:T(8,128)} %fusion.40, bf16[1024,512]{1,0:T(8,128)(2,1)S(1)} %copy-done.3, bf16[1024,2048]{1,0:T(8,128)(2,1)} %all-gather.8.cloned.1.call-done), kind=kOutput, calls=%fused_computation.17 | convolution fusion | flops 2148532224 | bytes 13631488 | tf_op jit(solution)/shard_map/dot_general | solution.py:32
  181.0 0.0 all-reduce.6.cloned.1.call-update
  181.1 0.0 all-gather.12.cloned.1.call-start
  181.1 0.5 all-gather.12.cloned.1.call-update
  181.7 0.0 all-reduce.4.cloned.1.call-start
  181.7 0.0 copy-start.1
  181.7 3.0 convert_reduce_fusion
  184.7 0.5 copy-done.1
  185.2 0.6 convert_reduce_fusion.1
  185.8 25.6 %all-reduce = (f32[2048]{0:T(1024)S(1)}, f32[2048]{0:T(1024)S(1)}) all-reduce(f32[2048]{0:T(1024)S(1)} %convert_reduce_fusion, f32[2048]{0:T(1024)S(1)} %convert_reduce_fusion.1), channel_id=1, replica_groups=mesh['rows'=8,'feat'=4] {'rows'}, use_global_device_ids=true, to_apply=%region_3.0 | all-reduce | flops 4096 | bytes 32768 | tf_op jit(solution)/shard_map/psum | solution.py:40
  211.4 0.1 dynamic_slice.10
  211.5 0.1 dynamic_slice.11
  211.6 7.4 %all-gather.10.cloned.1.call-done = f32[2048,256]{1,0:T(8,128)} async-done(((f32[512,256]{1,0:T(8,128)}), f32[2048,256]{1,0:T(8,128)}) %all-gather.10.cloned.1.call-update) | async-done | bytes 2097168 | tf_op jit(solution)/shard_map/all_gather | solution.py:52
  219.0 82.8 %all-reduce.6.cloned.1.call-done = f32[512,2048]{1,0:T(8,128)} async-done(((f32[512,2048]{1,0:T(8,128)}), f32[512,2048]{1,0:T(8,128)}) %all-reduce.6.cloned.1.call-update) | async-done | bytes 4194320 | tf_op jit(solution)/shard_map/psum | solution.py:40
  301.7 6.9 %fusion.6 = f32[512,256]{1,0:T(8,128)S(1)} fusion(f32[2048,256]{1,0:T(8,128)} %all-gather.10.cloned.1.call-done, f32[512,2048]{1,0:T(8,128)} %all-reduce.6.cloned.1.call-done, f32[2048]{0:T(1024)S(1)} %get-tuple-element.11, f32[512]{0:T(512)S(1)} %dynamic_slice.11, f32[2048]{0:T(1024)S(1)} %get-tuple-element.12, f32[512]{0:T(512)S(1)} %dynamic_slice.10), kind=kOutput, calls=%fused_computation.8 | convolution fusion | flops 3227516928 | bytes 6836224 | tf_op jit(solution)/shard_map/dot_general | solution.py:55
  308.6 0.0 copy-start.5
  308.6 32.3 %all-gather.12.cloned.1.call-done = f32[512,2048]{1,0:T(8,128)} async-done(((f32[512,256]{1,0:T(8,128)}), f32[512,2048]{1,0:T(8,128)}) %all-gather.12.cloned.1.call-update) | async-done | bytes 4194320 | tf_op jit(solution)/shard_map/all_gather | solution.py:53
  340.9 10.2 %convolution_bitcast_fusion = f32[2048,256]{1,0:T(8,128)} fusion(f32[512,256]{1,0:T(8,128)S(1)} %fusion.6, f32[512,2048]{1,0:T(8,128)} %all-gather.12.cloned.1.call-done), kind=kOutput, calls=%fused_computation.18 | convolution fusion | flops 3221225472 | bytes 6815744 | tf_op jit(solution)/shard_map/dot_general | solution.py:56
  351.1 0.0 all-reduce.4.cloned.1.call-update
  351.1 0.3 reduce-scatter.2.cloned.1.call-start
  351.4 0.0 copy-done.5
  351.4 0.1 broadcast_power_fusion.1
  351.5 85.9 %all-reduce.4.cloned.1.call-done = f32[2048,256]{1,0:T(8,128)} async-done(((f32[2048,256]{1,0:T(8,128)}), f32[2048,256]{1,0:T(8,128)}) %all-reduce.4.cloned.1.call-update) | async-done | bytes 2097168 | tf_op jit(solution)/shard_map/psum | solution.py:57
  437.4 10.8 %fusion.15 = f32[256,512]{1,0:T(8,128)S(1)} fusion(f32[512,2048]{1,0:T(8,128)} %all-gather.12.cloned.1.call-done, f32[2048,256]{1,0:T(8,128)} %all-reduce.4.cloned.1.call-done, f32[256]{0:T(256)S(1)} %get-tuple-element.8, f32[2048]{0:T(1024)S(1)} %copy-done.5, f32[256]{0:T(256)S(1)} %get-tuple-element.7, f32[2048]{0:T(1024)S(1)} %get-tuple-element.10, ...), kind=kOutput, calls=%fused_computation.20 | convolution fusion | flops 3224895488 | bytes 6843392 | tf_op jit(solution)/shard_map/dot_general | solution.py:61
  448.2 0.0 copy-done.4
  448.2 8.4 %fusion.41 = f32[512,2048]{1,0:T(8,128)} fusion(f32[256,512]{1,0:T(8,128)S(1)} %fusion.15, f32[2048,256]{1,0:T(8,128)S(1)} %copy-done.4), kind=kOutput, calls=%fused_computation.52 | convolution fusion | flops 3221225472 | bytes 6815744 | tf_op jit(solution)/shard_map/dot_general | solution.py:63
  456.6 0.0 reduce-scatter.2.cloned.1.call-update
  456.7 0.3 all-gather.14.cloned.1.call-start
  457.0 50.0 %reduce-scatter.2.cloned.1.call-done = f32[64,2048]{1,0:T(8,128)} async-done(((f32[512,2048]{1,0:T(8,128)}), f32[64,2048]{1,0:T(8,128)}) %reduce-scatter.2.cloned.1.call-update) | async-done | bytes 524304 | tf_op jit(solution)/shard_map/reduce_scatter | solution.py:62
  507.0 1.8 multiply_convert_fusion
  508.8 0.0 all-gather.14.cloned.1.call-update
  508.8 27.9 %all-gather.14.cloned.1.call-done = bf16[512,2048]{1,0:T(8,128)(2,1)} async-done(((bf16[64,2048]{1,0:T(8,128)(2,1)}), bf16[512,2048]{1,0:T(8,128)(2,1)}) %all-gather.14.cloned.1.call-update) | async-done | bytes 2097168 | tf_op jit(solution)/shard_map/all_gather | solution.py:69
  536.7 5.4 fusion.2
  542.1 0.0 copy-done
  542.1 3.3 add_convert_fusion
  (6 shorter events, 0.0 us)
Async XLA Ops:
  6.5 535.6 %copy-start = (bf16[2048,512]{1,0:T(8,128)(2,1)S(1)}, bf16[2048,512]{1,0:T(8,128)(2,1)}, u32[]{:S(2)}) copy-start(bf16[2048,512]{1,0:T(8,128)(2,1)} %param.9) | copy-start | bytes 6291460
  6.5 85.9 %all-gather.6.cloned.1.call-start = ((), (), s32[]{:S(2)}) async-start(), calls=%async_computation.1 | async-start | bytes 5242880 | tf_op jit(solution)/shard_map/all_gather | solution.py:71
  7.3 166.0 %all-gather.8.cloned.1.call-start = ((), (), s32[]{:S(2)}) async-start(), calls=%async_computation.2 | async-start | bytes 5242880 | tf_op jit(solution)/shard_map/all_gather | solution.py:70
  8.0 211.0 %all-gather.10.cloned.1.call-start = ((), (), s32[]{:S(2)}) async-start(), calls=%async_computation.3 | async-start | bytes 2621440 | tf_op jit(solution)/shard_map/all_gather | solution.py:52
  8.7 164.5 %copy-start.3 = (bf16[1024,512]{1,0:T(8,128)(2,1)S(1)}, bf16[1024,512]{1,0:T(8,128)(2,1)}, u32[]{:S(2)}) copy-start(bf16[1024,512]{1,0:T(8,128)(2,1)} %param.6) | copy-start | bytes 3145732
  8.8 293.0 %all-reduce.6.cloned.1.call-start = ((), (), s32[]{:S(2)}) async-start(), calls=%async_computation.8 | async-start | bytes 8388608 | tf_op jit(solution)/shard_map/psum | solution.py:40
  181.1 159.9 %all-gather.12.cloned.1.call-start = ((), (), s32[]{:S(2)}) async-start(), calls=%async_computation.4 | async-start | bytes 4718592 | tf_op jit(solution)/shard_map/all_gather | solution.py:53
  181.7 255.8 %all-reduce.4.cloned.1.call-start = ((), (), s32[]{:S(2)}) async-start(), calls=%async_computation.5 | async-start | bytes 4194304 | tf_op jit(solution)/shard_map/psum | solution.py:57
  181.7 3.5 copy-start.1
  308.6 42.8 %copy-start.5 = (f32[2048]{0:T(1024)S(1)}, f32[2048]{0:T(1024)}, u32[]{:S(2)}) copy-start(f32[2048]{0:T(1024)} %param.8) | copy-start | bytes 24580
  351.1 155.9 %reduce-scatter.2.cloned.1.call-start = ((), (), s32[]{:S(2)}) async-start(), calls=%async_computation.6 | async-start | bytes 4718592 | tf_op jit(solution)/shard_map/reduce_scatter | solution.py:62
  437.4 10.8 %copy-start.4 = (f32[2048,256]{1,0:T(8,128)S(1)}, f32[2048,256]{1,0:T(8,128)}, u32[]{:S(2)}) copy-start(f32[2048,256]{1,0:T(8,128)} %all-gather.10.cloned.1.call-done) | copy-start | bytes 6291460
  456.7 80.1 %all-gather.14.cloned.1.call-start = ((), (), s32[]{:S(2)}) async-start(), calls=%async_computation.7 | async-start | bytes 2359296 | tf_op jit(solution)/shard_map/all_gather | solution.py:69
  536.7 5.4 copy-start.2
Sparse Core Ops, SparseCore 0:
  8.9 83.4 all-gather.5
  94.0 79.2 all-gather.7
  174.8 44.1 all-gather.9
  222.1 79.5 all-reduce.5
  303.5 37.3 all-gather.11
  351.3 86.1 all-reduce.3
  456.8 50.1 reduce-scatter.1
  508.9 27.7 all-gather.13
where the time goes:
time: 552 us
  waiting for transfers between devices  447 us (81%)
  matrix products  59.6 us (11%)
  blocking collectives  25.6 us (5%)
  between operations  13.6 us (2%)
    psum x1, waiting for transfers between devices, local(): rotated = lax.psum(partial_value, 'feat')  85.9 us
    all_gather x1, waiting for transfers between devices, local(): piece_g = lax.all_gather(grad_out, 'feat', axis=1, tiled=True)  83.6 us
    psum x1, waiting for transfers between devices, local(): lax.psum((cross_one, cross_two, sum_x, sum_g), 'rows')  82.8 us
    all_gather x1, waiting for transfers between devices, local(): piece_x = lax.all_gather(features, 'feat', axis=1, tiled=True)  74 us
    reduce_scatter x1, waiting for transfers between devices, local(): lax.psum_scatter(lax.dot_general(back_rot, basis_cols, contract_last, pre...  50 us
    all_gather x1, waiting for transfers between devices, local(): basis_block = lax.all_gather(eigvecs, 'rows', axis=1, tiled=True)  32.3 us
    all_gather x1, waiting for transfers between devices, local(): sens_scaled = lax.all_gather(scaled_own, 'rows', axis=0, tiled=True)  27.9 us
    psum x1, blocking collectives, local(): lax.psum((cross_one, cross_two, sum_x, sum_g), 'rows')  25.6 us
  transfers between devices with their start and end apart: 8, of which 8 were waited for; matrix products, arithmetic and copies ran while one was open for 5% of the time, Pallas kernels for 0%

commit v1 on v0

--- a/solution.py
+++ b/solution.py
@@ -67,7 +67,7 @@
     )
     scaled_own = (2.0 / row_count * sens_own).astype(jnp.bfloat16)
     sens_scaled = lax.all_gather(scaled_own, "rows", axis=0, tiled=True)
-    piece_x = lax.all_gather(features, "feat", axis=1, tiled=True)
+    piece_x = jnp.concatenate(lax.all_gather(features, "feat"), axis=1)
     piece_g = lax.all_gather(grad_out, "feat", axis=1, tiled=True)
     shifted = (piece_g.astype(jnp.float32) - grad_mean).astype(jnp.bfloat16)
     centered = (piece_x.astype(jnp.float32) - col_mean).astype(jnp.bfloat16)

time: 552 us -> 627 us (1.14)
  waiting for transfers between devices: 447 us -> 506 us
  other arithmetic: 5.43 us -> 17.9 us
  local copies, waits for them, and re-layouts: 0.75 us -> 9.52 us
  matrix products: 59.6 us -> 53.3 us
    all_gather x0 -> x1, waiting for transfers between devices: none -> 80.6 us  [local(): piece_x = jnp.concatenate(lax.all_gather(features, 'feat'), axis=1)]
    all_gather x1, waiting for transfers between devices: 27.9 us -> 6.96 us  [local(): sens_scaled = lax.all_gather(scaled_own, 'rows', axis=0, tiled=True)]
    convert_element_type x0 -> x2, other arithmetic: none -> 12.5 us  [local(): centered = (piece_x.astype(jnp.float32) - col_mean).astype(jnp.bfloat16)]
    convert_element_type x0 -> x1, local copies, waits for them, and re-layouts: none -> 8.77 us  [local(): centered = (piece_x.astype(jnp.float32) - col_mean).astype(jnp.bfloat16)]
  transfers between devices with their start and end apart: 8 -> 9, of which waited for: 8 -> 9; matrix products, arithmetic and copies ran while one was open for 5% -> 8% of each run, Pallas kernels for 0% -> 0%
where the time goes in v1:
time: 627 us
  waiting for transfers between devices  506 us (81%)
  matrix products  53.3 us (9%)
  blocking collectives  25.6 us (4%)
  other arithmetic  17.9 us (3%)
  between operations  13.3 us (2%)
  local copies, waits for them, and re-layouts  9.52 us (2%)
    psum x1, waiting for transfers between devices, local(): rotated = lax.psum(partial_value, 'feat')  85.9 us
    all_gather x1, waiting for transfers between devices, local(): piece_g = lax.all_gather(grad_out, 'feat', axis=1, tiled=True)  83.6 us
    psum x1, waiting for transfers between devices, local(): lax.psum((cross_one, cross_two, sum_x, sum_g), 'rows')  82.8 us
    all_gather x1, waiting for transfers between devices, local(): piece_x = jnp.concatenate(lax.all_gather(features, 'feat'), axis=1)  80.6 us
    all_gather x1, waiting for transfers between devices, local(): piece_x = lax.all_gather(features, 'feat', axis=1, tiled=True)  74 us
    reduce_scatter x1, waiting for transfers between devices, local(): lax.psum_scatter(lax.dot_general(back_rot, basis_cols, contract_last, pre...  49.5 us
    all_gather x1, waiting for transfers between devices, local(): basis_block = lax.all_gather(eigvecs, 'rows', axis=1, tiled=True)  32.3 us
    psum x1, blocking collectives, local(): lax.psum((cross_one, cross_two, sum_x, sum_g), 'rows')  25.6 us
  transfers between devices with their start and end apart: 9, of which 9 were waited for; matrix products, arithmetic and copies ran while one was open for 8% of the time, Pallas kernels for 0%

profile of v1, /device:TPU:0, one launch (start us, length us, event | category | flops | bytes accessed | tf_op | source)
XLA Modules:
  0.0 626.6 jit_solution(15199631131642859101)
XLA Ops:
  6.5 0.0 all-gather.8.cloned.1.call-start
  6.5 0.7 all-gather.8.cloned.1.call-update
  7.3 0.0 all-gather.10.cloned.1.call-start
  7.3 0.7 all-gather.10.cloned.1.call-update
  8.0 0.0 all-gather.12.cloned.1.call-start
  8.1 0.7 all-gather.12.cloned.1.call-update
  8.8 0.0 all-reduce.6.cloned.1.call-start
  8.8 83.6 %all-gather.8.cloned.1.call-done = bf16[1024,2048]{1,0:T(8,128)(2,1)} async-done(((bf16[1024,512]{1,0:T(8,128)(2,1)}), bf16[1024,2048]{1,0:T(8,128)(2,1)}) %all-gather.8.cloned.1.call-update) | async-done | bytes 4194320 | tf_op jit(solution)/shard_map/all_gather | solution.py:71
  92.4 6.8 %fusion.37 = f32[512,2048]{1,0:T(8,128)} fusion(bf16[1024,512]{1,0:T(8,128)(2,1)} %param.5, bf16[1024,2048]{1,0:T(8,128)(2,1)} %all-gather.8.cloned.1.call-done), kind=kOutput, calls=%fused_computation.50 | convolution fusion | flops 2147483648 | bytes 9437184 | tf_op jit(solution)/shard_map/dot_general | solution.py:29
  99.2 74.0 %all-gather.10.cloned.1.call-done = bf16[1024,2048]{1,0:T(8,128)(2,1)} async-done(((bf16[1024,512]{1,0:T(8,128)(2,1)}), bf16[1024,2048]{1,0:T(8,128)(2,1)}) %all-gather.10.cloned.1.call-update) | async-done | bytes 4194320 | tf_op jit(solution)/shard_map/all_gather | solution.py:27
  173.2 7.8 %convolution_add_fusion = f32[512,2048]{1,0:T(8,128)} fusion(f32[512,2048]{1,0:T(8,128)} %fusion.37, bf16[1024,512]{1,0:T(8,128)(2,1)S(1)} %copy-done.3, bf16[1024,2048]{1,0:T(8,128)(2,1)} %all-gather.10.cloned.1.call-done), kind=kOutput, calls=%fused_computation.16 | convolution fusion | flops 2148532224 | bytes 13631488 | tf_op jit(solution)/shard_map/dot_general | solution.py:32
  181.0 0.0 all-reduce.6.cloned.1.call-update
  181.0 0.0 all-gather.14.cloned.1.call-start
  181.1 0.5 all-gather.14.cloned.1.call-update
  181.6 0.0 all-reduce.4.cloned.1.call-start
  181.7 3.0 convert_reduce_fusion
  184.7 0.5 copy-done.2
  185.2 0.6 convert_reduce_fusion.1
  185.8 25.6 %all-reduce = (f32[2048]{0:T(1024)S(1)}, f32[2048]{0:T(1024)S(1)}) all-reduce(f32[2048]{0:T(1024)S(1)} %convert_reduce_fusion.1, f32[2048]{0:T(1024)S(1)} %convert_reduce_fusion), channel_id=1, replica_groups=mesh['rows'=8,'feat'=4] {'rows'}, use_global_device_ids=true, to_apply=%region_3.0 | all-reduce | flops 4096 | bytes 32768 | tf_op jit(solution)/shard_map/psum | solution.py:40
  211.4 0.1 dynamic_slice.10
  211.5 0.1 dynamic_slice.11
  211.5 7.4 %all-gather.12.cloned.1.call-done = f32[2048,256]{1,0:T(8,128)} async-done(((f32[512,256]{1,0:T(8,128)}), f32[2048,256]{1,0:T(8,128)}) %all-gather.12.cloned.1.call-update) | async-done | bytes 2097168 | tf_op jit(solution)/shard_map/all_gather | solution.py:52
  219.0 82.8 %all-reduce.6.cloned.1.call-done = f32[512,2048]{1,0:T(8,128)} async-done(((f32[512,2048]{1,0:T(8,128)}), f32[512,2048]{1,0:T(8,128)}) %all-reduce.6.cloned.1.call-update) | async-done | bytes 4194320 | tf_op jit(solution)/shard_map/psum | solution.py:40
  301.7 6.9 %fusion.4 = f32[512,256]{1,0:T(8,128)S(1)} fusion(f32[2048,256]{1,0:T(8,128)} %all-gather.12.cloned.1.call-done, f32[512,2048]{1,0:T(8,128)} %all-reduce.6.cloned.1.call-done, f32[2048]{0:T(1024)S(1)} %get-tuple-element.11, f32[512]{0:T(512)S(1)} %dynamic_slice.11, f32[2048]{0:T(1024)S(1)} %get-tuple-element.12, f32[512]{0:T(512)S(1)} %dynamic_slice.10), kind=kOutput, calls=%fused_computation.8 | convolution fusion | flops 3227516928 | bytes 6836224 | tf_op jit(solution)/shard_map/dot_general | solution.py:55
  308.6 0.0 copy-start.5
  308.6 32.3 %all-gather.14.cloned.1.call-done = f32[512,2048]{1,0:T(8,128)} async-done(((f32[512,256]{1,0:T(8,128)}), f32[512,2048]{1,0:T(8,128)}) %all-gather.14.cloned.1.call-update) | async-done | bytes 4194320 | tf_op jit(solution)/shard_map/all_gather | solution.py:53
  340.9 7.1 %convolution_bitcast_fusion = f32[2048,256]{0,1:T(8,128)} fusion(f32[512,256]{1,0:T(8,128)S(1)} %fusion.4, f32[512,2048]{1,0:T(8,128)} %all-gather.14.cloned.1.call-done), kind=kOutput, calls=%fused_computation.17 | convolution fusion | flops 3221225472 | bytes 6815744 | tf_op jit(solution)/shard_map/dot_general | solution.py:56
  348.1 0.0 all-reduce.4.cloned.1.call-update
  348.1 0.3 reduce-scatter.2.cloned.1.call-start
  348.4 0.1 broadcast_power_fusion.1
  348.5 85.9 %all-reduce.4.cloned.1.call-done = f32[2048,256]{0,1:T(8,128)} async-done(((f32[2048,256]{0,1:T(8,128)}), f32[2048,256]{0,1:T(8,128)}) %all-reduce.4.cloned.1.call-update) | async-done | bytes 2097168 | tf_op jit(solution)/shard_map/psum | solution.py:57
  434.4 7.6 %fusion.12 = f32[256,512]{1,0:T(8,128)S(1)} fusion(f32[512,2048]{1,0:T(8,128)} %all-gather.14.cloned.1.call-done, f32[2048,256]{0,1:T(8,128)} %all-reduce.4.cloned.1.call-done, f32[256]{0:T(256)S(1)} %get-tuple-element.8, f32[2048]{0:T(1024)S(1)} %copy-done.5, f32[256]{0:T(256)S(1)} %get-tuple-element.7, f32[2048]{0:T(1024)S(1)} %get-tuple-element.10, ...), kind=kOutput, calls=%fused_computation.19 | convolution fusion | flops 3224895488 | bytes 6843392 | tf_op jit(solution)/shard_map/dot_general | solution.py:61
  442.0 0.0 copy-done.4
  442.0 8.5 %fusion.38 = f32[512,2048]{1,0:T(8,128)} fusion(f32[256,512]{1,0:T(8,128)S(1)} %fusion.12, f32[2048,256]{1,0:T(8,128)S(1)} %copy-done.4), kind=kOutput, calls=%fused_computation.51 | convolution fusion | flops 3221225472 | bytes 6815744 | tf_op jit(solution)/shard_map/dot_general | solution.py:63
  450.4 0.0 reduce-scatter.2.cloned.1.call-update
  450.5 0.0 all-gather.18.cloned.1.call-start
  450.5 0.7 all-gather.18.cloned.1.call-update
  451.2 0.0 all-gather.16.cloned.1.call-start
  451.3 49.5 %reduce-scatter.2.cloned.1.call-done = f32[64,2048]{1,0:T(8,128)} async-done(((f32[512,2048]{1,0:T(8,128)}), f32[64,2048]{1,0:T(8,128)}) %reduce-scatter.2.cloned.1.call-update) | async-done | bytes 524304 | tf_op jit(solution)/shard_map/reduce_scatter | solution.py:62
  500.8 1.8 multiply_convert_fusion
  502.6 0.0 all-gather.16.cloned.1.call-update
  502.6 80.6 %all-gather.18.cloned.1.call-done = bf16[4096,512]{1,0:T(8,128)(2,1)} async-done(((bf16[1024,512]{1,0:T(8,128)(2,1)}), bf16[4096,512]{1,0:T(8,128)(2,1)}) %all-gather.18.cloned.1.call-update) | async-done | bytes 4194320 | tf_op jit(solution)/shard_map/all_gather | solution.py:70
  583.2 6.6 %convert_bitcast_fusion = f32[1024,4,512]{2,0,1:T(8,128)} fusion(bf16[4,1024,512]{2,1,0:T(8,128)(2,1)} %bitcast.23), kind=kLoop, calls=%fused_computation.3 | loop fusion | flops 2097152 | bytes 12582912 | tf_op jit(solution)/shard_map/convert_element_type | solution.py:73
  589.8 8.8 %copy.6 = f32[1024,4,512]{0,2,1:T(8,128)} copy(f32[1024,4,512]{2,0,1:T(8,128)} %convert_bitcast_fusion) | data formatting | bytes 16777216 | tf_op jit(solution)/shard_map/convert_element_type | solution.py:73
  598.6 5.8 fusion.1
  604.4 7.0 %all-gather.16.cloned.1.call-done = bf16[512,2048]{1,0:T(8,128)(2,1)} async-done(((bf16[64,2048]{1,0:T(8,128)(2,1)}), bf16[512,2048]{1,0:T(8,128)(2,1)}) %all-gather.16.cloned.1.call-update) | async-done | bytes 2097168 | tf_op jit(solution)/shard_map/all_gather | solution.py:69
  611.4 5.4 fusion.39
  616.8 3.3 add_convert_fusion
  (12 shorter events, 0.0 us)
Async XLA Ops:
  6.5 610.2 %copy-start = (bf16[2048,512]{1,0:T(8,128)(2,1)S(1)}, bf16[2048,512]{1,0:T(8,128)(2,1)}, u32[]{:S(2)}) copy-start(bf16[2048,512]{1,0:T(8,128)(2,1)} %param.9) | copy-start | bytes 6291460
  6.5 85.9 %all-gather.8.cloned.1.call-start = ((), (), s32[]{:S(2)}) async-start(), calls=%async_computation.1 | async-start | bytes 5242880 | tf_op jit(solution)/shard_map/all_gather | solution.py:71
  7.3 166.0 %all-gather.10.cloned.1.call-start = ((), (), s32[]{:S(2)}) async-start(), calls=%async_computation.2 | async-start | bytes 5242880 | tf_op jit(solution)/shard_map/all_gather | solution.py:27
  8.0 211.0 %all-gather.12.cloned.1.call-start = ((), (), s32[]{:S(2)}) async-start(), calls=%async_computation.3 | async-start | bytes 2621440 | tf_op jit(solution)/shard_map/all_gather | solution.py:52
  8.7 164.5 %copy-start.3 = (bf16[1024,512]{1,0:T(8,128)(2,1)S(1)}, bf16[1024,512]{1,0:T(8,128)(2,1)}, u32[]{:S(2)}) copy-start(bf16[1024,512]{1,0:T(8,128)(2,1)} %param.6) | copy-start | bytes 3145732
  8.8 293.0 %all-reduce.6.cloned.1.call-start = ((), (), s32[]{:S(2)}) async-start(), calls=%async_computation.9 | async-start | bytes 8388608 | tf_op jit(solution)/shard_map/psum | solution.py:40
  181.0 159.9 %all-gather.14.cloned.1.call-start = ((), (), s32[]{:S(2)}) async-start(), calls=%async_computation.4 | async-start | bytes 4718592 | tf_op jit(solution)/shard_map/all_gather | solution.py:53
  181.6 252.8 %all-reduce.4.cloned.1.call-start = ((), (), s32[]{:S(2)}) async-start(), calls=%async_computation.5 | async-start | bytes 4194304 | tf_op jit(solution)/shard_map/psum | solution.py:57
  181.7 3.5 copy-start.2
  308.6 39.7 %copy-start.5 = (f32[2048]{0:T(1024)S(1)}, f32[2048]{0:T(1024)}, u32[]{:S(2)}) copy-start(f32[2048]{0:T(1024)} %param.8) | copy-start | bytes 24580
  348.1 152.7 %reduce-scatter.2.cloned.1.call-start = ((), (), s32[]{:S(2)}) async-start(), calls=%async_computation.6 | async-start | bytes 4718592 | tf_op jit(solution)/shard_map/reduce_scatter | solution.py:62
  434.4 7.6 %copy-start.4 = (f32[2048,256]{1,0:T(8,128)S(1)}, f32[2048,256]{1,0:T(8,128)}, u32[]{:S(2)}) copy-start(f32[2048,256]{1,0:T(8,128)} %all-gather.12.cloned.1.call-done) | copy-start | bytes 6291460
  450.5 132.7 %all-gather.18.cloned.1.call-start = ((), (), s32[]{:S(2)}) async-start(), calls=%async_computation.8 | async-start | bytes 5242880 | tf_op jit(solution)/shard_map/all_gather | solution.py:70
  451.2 160.1 %all-gather.16.cloned.1.call-start = ((), (), s32[]{:S(2)}) async-start(), calls=%async_computation.7 | async-start | bytes 2359296 | tf_op jit(solution)/shard_map/all_gather | solution.py:69
  611.4 5.4 copy-start.1
Sparse Core Ops, SparseCore 0:
  8.9 83.4 all-gather.7
  94.0 79.2 all-gather.9
  174.8 44.1 all-gather.11
  222.1 79.5 all-reduce.5
  303.5 37.3 all-gather.13
  348.2 86.1 all-reduce.3
  450.6 50.1 reduce-scatter.1
  502.4 80.7 all-gather.17
  585.1 26.2 all-gather.15
